TPU v7x, 32 devices: a whole 2x2x4 slice. The times are simulated.
32 devices in a mesh: seq: 16 (over z, x, core), ch: 2 (over y).
Axes of the slice: x: 2, y: 2, z: 4, core: 2. Of those that a mesh axis runs over, the one named last changes fastest.
Arguments:
- out_grad: bfloat16 [2048, 4096], P('seq', 'ch'), may hold values from -6 to 6
- out_weight: bfloat16 [4096, 4096], P(('seq', 'ch')), may hold values from -0.09375 to 0.09375
- outer_gate: bfloat16 [2048, 4096], P('seq', 'ch'), may hold values from -6 to 6
- long_out: bfloat16 [2048, 4096], P('seq', 'ch'), may hold values from -6 to 6
- inner_gate: bfloat16 [2048, 4096], P('seq', 'ch'), may hold values from -6 to 6
- conv_input: bfloat16 [2048, 4096], P('seq', 'ch'), may hold values from -6 to 6
- short_out: bfloat16 [2048, 4096], P('seq', 'ch'), may hold values from -6 to 6
- medium_out: bfloat16 [2048, 4096], P('seq', 'ch'), may hold values from -6 to 6
- long_filter: bfloat16 [2048, 4096], P('seq', 'ch'), may hold values from -6 to 6
- taps_short: bfloat16 [7, 4096], P(None, 'ch'), may hold values from -2 to 2
- taps_medium: bfloat16 [128, 4096], P(None, 'ch'), may hold values from -0.5 to 0.5
Outputs:
- grad_outer: bfloat16 [2048, 4096], P('seq', 'ch')
- grad_inner: bfloat16 [2048, 4096], P('seq', 'ch')
- grad_input: bfloat16 [2048, 4096], P('seq', 'ch')
- grad_filter: float32 [2048, 4096], P('seq', 'ch')
- grad_short: float32 [7, 4096], P(None, 'ch')
- grad_medium: float32 [128, 4096], P(None, 'ch')
All inputs are finite; a program needn't handle non-finite values.
Results may differ from a plain program's by a relative error of at most 0.0065.
Values may be sent and summed in bfloat16 or wider, within the bound.
No kernel may reach another device: no remote copies, remote signals or barrier semaphores. Data moves between devices by JAX's collectives and lax.ppermute only.
A program may use at most 128 MiB of HBM per device.

v0:
```python
import math
import jax
import jax.numpy as jnp
from jax import lax
from jax.sharding import PartitionSpec as P

SHORT = 7
MEDIUM = 128
ACCURATE = lax.Precision.HIGH


def from_behind(value, axis, steps):
    count = lax.axis_size(axis)
    leading, last = (max(0, -steps), min(count, count - steps))
    return lax.ppermute(value, axis, [(source, source + steps) for source in range(leading, last)])


def rotation(numer, denom):
    angles = 2.0 * math.pi / denom * numer.astype(jnp.float32)
    return (jnp.cos(angles), jnp.sin(angles))


def dft_table(length, orient):
    indices = lax.iota(jnp.int32, length)
    cosine, sine_part = rotation(indices[:, None] * indices[None, :] % length, length)
    return (cosine, orient * sine_part)


def apply_table(table, real_part, imag_part, pattern):

    def multiply(left, right):
        return jnp.einsum(pattern, left, right, precision=ACCURATE)

    if imag_part is None:
        return (multiply(table[0], real_part), multiply(table[1], real_part))
    return (
        multiply(table[0], real_part) - multiply(table[1], imag_part),
        multiply(table[0], imag_part) + multiply(table[1], real_part),
    )


def real_table(table, real_part, imag_part, pattern):
    return jnp.einsum(pattern, table[0], real_part, precision=ACCURATE) - jnp.einsum(
        pattern, table[1], imag_part, precision=ACCURATE
    )


def twist(real_part, imag_part, cosine, sine_part):
    return (real_part * cosine - imag_part * sine_part, real_part * sine_part + imag_part * cosine)


def outer_forward(signal, time_pos, row_pos, freq_pos, total):
    table = dft_table(signal.shape[0], -1.0)
    cosine, sine_part = rotation(time_pos, 2 * total)
    shift_real, shift_imag = rotation(row_pos * freq_pos % total, total)
    outputs = []
    for parity in range(2):
        if parity == 0:
            real_part, imag_part = apply_table(table, signal, None, "ca,am->cm")
        else:
            real_part, imag_part = apply_table(
                table, signal * cosine, -signal * sine_part, "ca,am->cm"
            )
        outputs += list(twist(real_part, imag_part, shift_real, -shift_imag))
    return outputs


def inner_forward(parts):
    table = dft_table(parts[0].shape[0], -1.0)
    outputs = []
    for place in range(0, len(parts), 2):
        outputs += list(apply_table(table, parts[place], parts[place + 1], "br,rn->bn"))
    return outputs


def inner_inverse(parts, narrow, total):
    table = dft_table(parts[0].shape[0], 1.0)
    row_pos = lax.iota(jnp.int32, parts[0].shape[0])[:, None]
    freq_pos = lax.iota(jnp.int32, parts[0].shape[1])[None, :] // narrow
    shift_real, shift_imag = rotation(row_pos * freq_pos % total, total)
    outputs = []
    for place in range(0, len(parts), 2):
        real_part, imag_part = apply_table(table, parts[place], parts[place + 1], "rb,bn->rn")
        outputs += list(twist(real_part, imag_part, shift_real, shift_imag))
    return outputs


def outer_inverse(parts, time_pos, total):
    table = dft_table(parts[0].shape[0], 1.0)
    cosine, sine_part = rotation(time_pos, 2 * total)
    outputs = []
    for place in range(0, len(parts), 4):
        high_real, high_imag = apply_table(table, parts[place + 2], parts[place + 3], "ac,cm->am")
        high_real, high_imag = twist(high_real, high_imag, cosine, sine_part)
        outputs.append(real_table(table, parts[place], parts[place + 1], "ac,cm->am") + high_real)
    return outputs


def conj_times(left_real, left_imag, right_real, right_imag):
    return (
        left_real * right_real + left_imag * right_imag,
        left_real * right_imag - left_imag * right_real,
    )


def spectral_terms(spectra):
    first, second = ([], [])
    for parity in range(2):
        grad_real, grad_imag = (spectra[4 + 2 * parity], spectra[5 + 2 * parity])
        point_real, point_imag = conj_times(
            spectra[8 + 2 * parity], spectra[9 + 2 * parity], grad_real, grad_imag
        )
        filt_real, filt_imag = conj_times(
            spectra[2 * parity], spectra[2 * parity + 1], grad_real, grad_imag
        )
        first += [point_real, point_imag]
        second += [filt_real, filt_imag]
    return first + second


def depthwise(signal, kernel):
    channels = signal.shape[1]
    result = lax.conv_general_dilated(
        signal.astype(jnp.float32)[None],
        kernel.astype(jnp.float32)[:, None, :],
        (1,),
        "VALID",
        dimension_numbers=("NWC", "WIO", "NWC"),
        feature_group_count=channels,
        precision=lax.Precision.HIGHEST,
    )
    return result[0]


def adjoint_taps(extended, taps):
    return depthwise(extended, taps)


def tap_products(grads, extended):
    return depthwise(extended, grads)[::-1]


def per_device(
    out_grad,
    out_weight,
    outer_gate,
    long_out,
    inner_gate,
    conv_input,
    short_out,
    medium_out,
    long_filter,
    taps_short,
    taps_medium,
):
    height = out_grad.shape[0]
    channels = outer_gate.shape[1]
    devices = lax.axis_size("seq")
    total = height * devices
    earlier_short, earlier_input = from_behind(
        (short_out[height - (MEDIUM - 1) :], conv_input[height - (SHORT - 1) :]), "seq", 1
    )
    features = lax.all_gather(out_grad, "ch", axis=1, tiled=True)
    aligned = lax.all_to_all(out_weight, "ch", split_axis=1, concat_axis=0, tiled=True)
    hidden = jnp.dot(
        features,
        lax.all_gather(aligned, "seq", axis=0, tiled=True),
        preferred_element_type=jnp.float32,
    )
    grad_outer = (hidden * long_out.astype(jnp.float32)).astype(jnp.bfloat16)
    long_grad = (hidden * outer_gate.astype(jnp.float32)).astype(jnp.bfloat16)
    product = (inner_gate.astype(jnp.float32) * medium_out.astype(jnp.float32)).astype(jnp.bfloat16)
    narrow = channels // devices
    lane_span = height * narrow

    def to_blocks(signal):
        return (
            signal.reshape(height, devices, narrow).transpose(1, 0, 2).reshape(devices, lane_span)
        )

    def to_inner(signal):
        return (
            signal.reshape(devices, height, narrow)
            .transpose(1, 0, 2)
            .reshape(height, devices * narrow)
        )

    arrived = (
        lax.all_to_all(to_blocks(product), "seq", split_axis=0, concat_axis=0, tiled=True),
        lax.all_to_all(to_blocks(long_grad), "seq", split_axis=0, concat_axis=0, tiled=True),
        lax.all_to_all(to_blocks(long_filter), "seq", split_axis=0, concat_axis=0, tiled=True),
    )
    row_pos = lax.iota(jnp.int32, lane_span)[None, :] // narrow
    source = lax.iota(jnp.int32, devices)[:, None]
    time_pos = source * height + row_pos
    spread = []
    for signal in arrived:
        spread += outer_forward(signal.astype(jnp.float32), time_pos, row_pos, source, total)
    spectra = inner_forward([to_inner(piece) for piece in spread])
    terms = inner_inverse(spectral_terms(spectra), narrow, total)
    results = outer_inverse([to_blocks(piece) for piece in terms], time_pos, total)
    result = lax.all_to_all(jnp.stack(results), "seq", split_axis=1, concat_axis=1, tiled=True)
    result = (
        result.reshape(2, devices, height, narrow)
        .transpose(0, 2, 1, 3)
        .reshape(2, height, channels)
    )
    scale = total ** (-0.5) / (2.0 * total)
    point_grad = result[0] * scale
    grad_filter = result[1] * scale
    medium_grad = (point_grad * inner_gate.astype(jnp.float32)).astype(jnp.bfloat16)
    grad_inner = (point_grad * medium_out.astype(jnp.float32)).astype(jnp.bfloat16)
    later_medium = from_behind(medium_grad[: MEDIUM - 1], "seq", -1)
    short_grad = adjoint_taps(jnp.concatenate([medium_grad, later_medium]), taps_medium).astype(
        jnp.bfloat16
    )
    later_short = from_behind(short_grad[: SHORT - 1], "seq", -1)
    grad_input = adjoint_taps(jnp.concatenate([short_grad, later_short]), taps_short).astype(
        jnp.bfloat16
    )
    partial_medium = tap_products(medium_grad, jnp.concatenate([earlier_short, short_out]))
    partial_short = tap_products(short_grad, jnp.concatenate([earlier_input, conv_input]))
    sum_medium, sum_short = lax.psum((partial_medium, partial_short), "seq")
    factor = total ** (-0.5)
    return (
        grad_outer,
        grad_inner,
        grad_input,
        grad_filter,
        sum_short * factor,
        sum_medium * factor,
    )


def solution(mesh):
    return jax.shard_map(
        per_device,
        mesh=mesh,
        in_specs=(
            P("seq", "ch"),
            P(("seq", "ch"), None),
            P("seq", "ch"),
            P("seq", "ch"),
            P("seq", "ch"),
            P("seq", "ch"),
            P("seq", "ch"),
            P("seq", "ch"),
            P("seq", "ch"),
            P(None, "ch"),
            P(None, "ch"),
        ),
        out_specs=(
            P("seq", "ch"),
            P("seq", "ch"),
            P("seq", "ch"),
            P("seq", "ch"),
            P(None, "ch"),
            P(None, "ch"),
        ),
        check_vma=False,
    )
```

profile of v0, /device:TPU:0, one launch (start us, length us, event | category | flops | bytes accessed | tf_op | source)
XLA Modules:
  0.0 585.1 jit_solution(104122376312642344)
XLA Ops:
  9.6 24.2 %all_to_all.63 = bf16[128,2,2048]{0,2,1:T(8,128)(2,1)S(1)} all-to-all(bf16[128,2,2048]{0,2,1:T(8,128)(2,1)S(1)} %bitcast.387), channel_id=1, replica_groups=mesh['seq'=16,'ch'=2] {'ch'}, dimensions={1} | all-to-all | bytes 2097152 | tf_op jit(solution)/shard_map/all_to_all | solution.py:164
  36.0 3.8 reduce
  41.0 6.4 %all-to-all-start.1 = ((bf16[16,2,8192]{2,1,0:T(2,128)(2,1)}), bf16[16,2,8192]{2,1,0:T(2,128)(2,1)S(1)}, u32[]{:S(2)}, u32[]{:S(2)}) async-start(bf16[16,2,8192]{2,1,0:T(2,128)(2,1)} %reshape.319), calls=%async_computation.1 | async-start | bytes 1048576 | tf_op jit(solution)/shard_map/all_to_all | solution.py:191
  48.8 3.8 reduce.2
  53.8 13.7 %all-to-all-done.1 = bf16[16,2,8192]{2,1,0:T(2,128)(2,1)S(1)} async-done(((bf16[16,2,8192]{2,1,0:T(2,128)(2,1)}), bf16[16,2,8192]{2,1,0:T(2,128)(2,1)S(1)}, u32[]{:S(2)}, u32[]{:S(2)}) %all-to-all-start.1) | async-done | bytes 524320 | tf_op jit(solution)/shard_map/all_to_all | solution.py:191
  67.6 11.8 %all-to-all-start.3 = ((bf16[16,2,8192]{2,1,0:T(2,128)(2,1)}), bf16[16,2,8192]{2,1,0:T(2,128)(2,1)S(1)}, u32[]{:S(2)}, u32[]{:S(2)}) async-start(bf16[16,2,8192]{2,1,0:T(2,128)(2,1)} %reshape.315), calls=%async_computation.3 | async-start | bytes 1048576 | tf_op jit(solution)/shard_map/all_to_all | solution.py:189
  80.5 21.9 %all-to-all-done.3 = bf16[16,2,8192]{2,1,0:T(2,128)(2,1)S(1)} async-done(((bf16[16,2,8192]{2,1,0:T(2,128)(2,1)}), bf16[16,2,8192]{2,1,0:T(2,128)(2,1)S(1)}, u32[]{:S(2)}, u32[]{:S(2)}) %all-to-all-start.3) | async-done | bytes 524320 | tf_op jit(solution)/shard_map/all_to_all | solution.py:189
  105.5 4.1 fusion.71
  109.6 5.1 fusion.56
  114.8 5.2 fusion.65
  119.9 5.5 fusion.58
  125.4 5.1 convolution_add_fusion.4
  130.5 56.4 %all-gather.5.cloned.1.call-done = bf16[4096,2048]{1,0:T(8,128)(2,1)} async-done(((bf16[256,2048]{1,0:T(8,128)(2,1)}), bf16[4096,2048]{1,0:T(8,128)(2,1)}) %all-gather.5.cloned.1.call-update) | async-done | bytes 16777232 | tf_op jit(solution)/shard_map/all_gather | solution.py:167
  186.9 9.4 %fusion.88 = (bf16[16,16,8,128]{3,2,1,0:T(8,128)(2,1)S(1)}, bf16[128,2048]{1,0:T(8,128)(2,1)}) fusion(bf16[128,2048]{1,0:T(8,128)(2,1)S(1)} %copy-done.50, bf16[128,2048]{1,0:T(8,128)(2,1)} %param.14, bf16[128,4096]{1,0:T(8,128)(2,1)} %all-gather.3.cloned.1.call-done, bf16[4096,2048]{1,0:T(8,128)(2,1)} %all-gather.5.cloned.1.call-done), kind=kOutput, calls=%fused_computation.181 | convolution fusion | flops 2149056512 | bytes 19922944 | tf_op jit(solution)/shard_map/dot_general | solution.py:165
  198.1 4.9 reduce.1
  204.2 4.2 all-to-all-start.2
  210.0 6.6 %convolution_subtract_fusion.5 = f32[16,16384]{1,0:T(8,128)} fusion(f32[16,16384]{1,0:T(8,128)} %fusion.56, bf16[16,1,16384]{2,0,1:T(8,128)(2,1)S(1)} %copy.177, s32[16]{0:T(128)S(1)} %iota_multiply_fusion, s32[16384]{0:T(1024)S(1)} %add_select_fusion.2), kind=kOutput, calls=%fused_computation.20 | convolution fusion | flops 27004672 | bytes 2687040 | tf_op jit(solution)/shard_map/ca,am->cm/dot_general | solution.py:32
  216.6 5.1 convolution_add_fusion.1
  221.7 5.2 convolution_subtract_fusion.1
  226.9 2.4 reshape.318
  230.8 4.1 fusion.68
  234.9 4.0 fusion.57
  239.0 4.3 convolution_add_fusion.3
  243.3 4.1 convolution_subtract_fusion.4
  247.5 8.8 %subtract_bitcast_fusion.6 = (f32[2,8,128,128]{3,1,2,0:T(8,128)}, f32[2,8,128,128]{3,1,2,0:T(8,128)}, f32[2,8,128,128]{3,1,2,0:T(8,128)}, f32[2,8,128,128]{3,1,2...) fusion(f32[16,16384]{1,0:T(8,128)S(1)} %copy-done.16, ...), kind=kOutput, calls=%fused_computation.139 | convolution fusion | flops 38538752 | bytes 24707072 | tf_op jit(solution)/shard_map/ca,am->cm/dot_general | solution.py:32
  259.2 1.8 fusion.186
  263.7 1.9 fusion.190
  265.6 1.8 convolution_add_fusion.10
  270.1 1.8 fusion.192
  274.7 1.8 fusion.188
  276.5 1.8 convolution_subtract_fusion.13
  278.3 1.8 convolution_subtract_fusion.12
  283.0 1.8 fusion.170
  291.7 2.8 multiply_add_fusion.2
  296.2 1.9 convolution_add_fusion.9
  298.0 1.9 convolution_subtract_fusion.11
  302.8 1.8 fusion.198
  307.4 1.9 fusion.202
  309.3 1.8 convolution_add_fusion.13
  313.8 1.8 fusion.204
  318.4 1.8 fusion.200
  320.2 1.8 convolution_subtract_fusion.16
  322.0 2.1 convolution_subtract_fusion.15
  327.0 1.8 fusion.178
  347.9 5.7 add_bitcast_fusion.4
  357.5 4.4 fusion.4
  365.7 4.8 fusion.9
  372.6 4.5 fusion.3
  377.1 4.7 fusion.8
  381.9 3.0 copy.165
  384.9 6.0 %all-to-all-start.4 = ((f32[2,16,16384]{2,0,1:T(2,128)}), f32[2,16,16384]{2,0,1:T(2,128)S(1)}, u32[]{:S(2)}, u32[]{:S(2)}) async-start(f32[2,16,16384]{2,0,1:T(2,128)} %copy.165), calls=%async_computation.4 | async-start | bytes 4194304 | tf_op jit(solution)/shard_map/all_to_all | solution.py:202
  391.1 2.3 collective-permute-start.3
  394.3 3.5 collective-permute-start.2
  398.6 2.0 maximum_bitcast_fusion.3
  401.7 30.2 %all-to-all-done.4 = f32[2,16,16384]{2,0,1:T(2,128)S(1)} async-done(((f32[2,16,16384]{2,0,1:T(2,128)}), f32[2,16,16384]{2,0,1:T(2,128)S(1)}, u32[]{:S(2)}, u32[]{:S(2)}) %all-to-all-start.4) | async-done | bytes 2097184 | tf_op jit(solution)/shard_map/all_to_all | solution.py:202
  431.9 2.8 reshape.304
  434.7 2.8 copy.296
  441.3 14.9 %fusion.11 = f32[1,128,2048]{2,0,1:T(1,128)S(1)} fusion(bf16[1,255,2048]{2,1,0:T(8,128)(2,1)S(1)} %copy-done.48, bf16[128,1,2048]{2,0,1:T(8,128)(2,1)S(1)} %bitcast.394), kind=kOutput, calls=%fused_computation.47 | convolution fusion | flops 67108864 | bytes 2617344 | tf_op jit(solution)/shard_map/conv_general_dilated | solution.py:123
  457.9 5.2 rev.7
  463.2 14.8 %convolution_convert_fusion = bf16[1,128,2048]{2,0,1:T(2,128)(2,1)S(1)} fusion(bf16[1,255,2048]{2,1,0:T(8,128)(2,1)S(1)} %maximum_bitcast_fusion, bf16[128,1,2048]{2,0,1:T(8,128)(2,1)S(1)} %bitcast.335), kind=kOutput, calls=%fused_computation.43 | convolution fusion | flops 67371008 | bytes 2093056 | tf_op jit(solution)/shard_map/conv_general_dilated | solution.py:123
  479.7 2.5 fusion.15
  482.6 68.9 %psum.14 = f32[7,2048]{1,0:T(8,128)S(1)} all-reduce(f32[7,2048]{1,0:T(8,128)S(1)} %rev.6), channel_id=1, replica_groups=mesh['seq'=16,'ch'=2] {'seq'}, use_global_device_ids=true, to_apply=%region_0.1 | all-reduce | flops 14336 | bytes 114688 | tf_op jit(solution)/shard_map/psum | solution.py:223
  552.2 21.0 %all-reduce.2.cloned.1.call-done = f32[128,2048]{1,0:T(8,128)} async-done(((f32[128,2048]{1,0:T(8,128)}), f32[128,2048]{1,0:T(8,128)}) %all-reduce.2.cloned.1.call-update) | async-done | bytes 1048592 | tf_op jit(solution)/shard_map/psum | solution.py:223
  573.2 2.3 broadcast_multiply_fusion
  (227 shorter events, 97.9 us)
Async XLA Ops:
  7.2 456.0 %copy-start = (bf16[128,2048]{1,0:T(8,128)(2,1)S(1)}, bf16[128,2048]{1,0:T(8,128)(2,1)}, u32[]{:S(2)}) copy-start(bf16[128,2048]{1,0:T(8,128)(2,1)} %param.21) | copy-start | bytes 1572868
  7.2 123.3 %all-gather.3.cloned.1.call-start = ((), (), s32[]{:S(2)}) async-start(), calls=%async_computation.5 | async-start | bytes 1572864 | tf_op jit(solution)/shard_map/all_gather | solution.py:163
  7.9 179.0 %all-gather.5.cloned.1.call-start = ((), (), s32[]{:S(2)}) async-start(), calls=%async_computation.6 | async-start | bytes 17825792 | tf_op jit(solution)/shard_map/all_gather | solution.py:167
  33.8 1.3 copy-start.51
  35.5 11.9 %copy-start.44 = (bf16[128,2048]{1,0:T(8,128)(2,1)S(1)}, bf16[128,2048]{1,0:T(8,128)(2,1)}, u32[]{:S(2)}) copy-start(bf16[128,2048]{1,0:T(8,128)(2,1)} %param.15) | copy-start | bytes 1572868
  41.0 26.6 %all-to-all-start.1 = ((bf16[16,2,8192]{2,1,0:T(2,128)(2,1)}), bf16[16,2,8192]{2,1,0:T(2,128)(2,1)S(1)}, u32[]{:S(2)}, u32[]{:S(2)}) async-start(bf16[16,2,8192]{2,1,0:T(2,128)(2,1)} %reshape.319), calls=%async_computation.1 | async-start | bytes 1048576 | tf_op jit(solution)/shard_map/all_to_all | solution.py:191
  67.6 34.9 %all-to-all-start.3 = ((bf16[16,2,8192]{2,1,0:T(2,128)(2,1)}), bf16[16,2,8192]{2,1,0:T(2,128)(2,1)S(1)}, u32[]{:S(2)}, u32[]{:S(2)}) async-start(bf16[16,2,8192]{2,1,0:T(2,128)(2,1)} %reshape.315), calls=%async_computation.3 | async-start | bytes 1048576 | tf_op jit(solution)/shard_map/all_to_all | solution.py:189
  119.9 67.0 %copy-start.50 = (bf16[128,2048]{1,0:T(8,128)(2,1)S(1)}, bf16[128,2048]{1,0:T(8,128)(2,1)}, u32[]{:S(2)}) copy-start(bf16[128,2048]{1,0:T(8,128)(2,1)} %param.13) | copy-start | bytes 1572868
  204.2 22.7 %all-to-all-start.2 = ((bf16[16,2,8192]{2,1,0:T(2,128)(2,1)}), bf16[16,2,8192]{2,1,0:T(2,128)(2,1)}, u32[]{:S(2)}, u32[]{:S(2)}) async-start(bf16[16,2,8192]{2,1,0:T(2,128)(2,1)} %reshape.317), calls=%async_computation.2 | async-start | bytes 1048576 | tf_op jit(solution)/shard_map/all_to_all | solution.py:190
  208.4 8.2 %copy-start.35 = (f32[16,16384]{1,0:T(8,128)S(1)}, f32[16,16384]{1,0:T(8,128)}, u32[]{:S(2)}) copy-start(f32[16,16384]{1,0:T(8,128)} %fusion.65) | copy-start | bytes 3145732
  210.0 11.7 %copy-start.34 = (f32[16,16384]{1,0:T(8,128)S(1)}, f32[16,16384]{1,0:T(8,128)}, u32[]{:S(2)}) copy-start(f32[16,16384]{1,0:T(8,128)} %fusion.58) | copy-start | bytes 3145732
  234.9 12.5 %copy-start.22 = (f32[16,16384]{1,0:T(8,128)S(1)}, f32[16,16384]{1,0:T(8,128)}, u32[]{:S(2)}) copy-start(f32[16,16384]{1,0:T(8,128)} %convolution_subtract_fusion.1) | copy-start | bytes 3145732
  239.0 8.4 %copy-start.15 = (f32[16,16384]{1,0:T(8,128)S(1)}, f32[16,16384]{1,0:T(8,128)}, u32[]{:S(2)}) copy-start(f32[16,16384]{1,0:T(8,128)} %fusion.96) | copy-start | bytes 3145732
  239.0 8.4 %copy-start.16 = (f32[16,16384]{1,0:T(8,128)S(1)}, f32[16,16384]{1,0:T(8,128)}, u32[]{:S(2)}) copy-start(f32[16,16384]{1,0:T(8,128)} %convolution_add_fusion.4) | copy-start | bytes 3145732
  239.0 8.4 %copy-start.19 = (f32[16,16384]{1,0:T(8,128)S(1)}, f32[16,16384]{1,0:T(8,128)}, u32[]{:S(2)}) copy-start(f32[16,16384]{1,0:T(8,128)} %fusion.110) | copy-start | bytes 3145732
  239.0 8.4 %copy-start.20 = (f32[16,16384]{1,0:T(8,128)S(1)}, f32[16,16384]{1,0:T(8,128)}, u32[]{:S(2)}) copy-start(f32[16,16384]{1,0:T(8,128)} %convolution_subtract_fusion.5) | copy-start | bytes 3145732
  239.0 8.4 %copy-start.21 = (f32[16,16384]{1,0:T(8,128)S(1)}, f32[16,16384]{1,0:T(8,128)}, u32[]{:S(2)}) copy-start(f32[16,16384]{1,0:T(8,128)} %convolution_add_fusion.1) | copy-start | bytes 3145732
  257.5 3.5 copy-start.25
  263.7 1.9 copy-start.29
  265.6 1.8 copy-start.24
  270.1 3.0 copy-start.5
  270.1 1.8 copy-start.23
  274.7 1.8 copy-start.30
  276.5 1.8 copy-start.26
  278.3 1.8 copy-start.18
  281.3 3.5 copy-start.17
  287.6 1.2 copy-start.31
  288.8 1.8 copy-start.41
  288.8 1.8 copy-start.43
  289.7 1.4 copy-start.6
  289.7 1.7 copy-start.37
  289.7 2.0 copy-start.39
  298.0 1.9 copy-start.14
  301.1 3.4 copy-start.13
  307.4 1.9 copy-start.32
  309.2 1.8 copy-start.12
  313.8 3.0 copy-start.3
  313.8 1.8 copy-start.11
  318.4 1.8 copy-start.33
  320.2 1.8 copy-start.27
  322.0 2.1 copy-start.10
  325.3 3.5 copy-start.9
  331.6 1.2 copy-start.28
  332.8 1.8 copy-start.40
  332.8 1.8 copy-start.42
  333.7 1.4 copy-start.4
  333.7 1.7 copy-start.36
  333.7 2.0 copy-start.38
  339.6 1.2 copy-start.1
  339.6 2.0 copy-start.2
  346.4 1.2 copy-start.7
  346.4 1.5 copy-start.8
  384.9 6.1 %copy-start.47 = (bf16[128,2048]{1,0:T(8,128)(2,1)S(1)}, bf16[128,2048]{1,0:T(8,128)(2,1)}, u32[]{:S(2)}) copy-start(bf16[128,2048]{1,0:T(8,128)(2,1)} %param.17) | copy-start | bytes 1572868
  384.9 47.0 %all-to-all-start.4 = ((f32[2,16,16384]{2,0,1:T(2,128)}), f32[2,16,16384]{2,0,1:T(2,128)S(1)}, u32[]{:S(2)}, u32[]{:S(2)}) async-start(f32[2,16,16384]{2,0,1:T(2,128)} %copy.165), calls=%async_computation.4 | async-start | bytes 4194304 | tf_op jit(solution)/shard_map/all_to_all | solution.py:202
  390.9 182.2 %all-reduce.2.cloned.1.call-start = ((), (), s32[]{:S(2)}) async-start(), calls=%async_computation.7 | async-start | bytes 2097152 | tf_op jit(solution)/shard_map/psum | solution.py:223
  391.1 9.5 %collective-permute-start.3 = (bf16[127,2048]{1,0:T(8,128)(2,1)S(1)}, bf16[127,2048]{1,0:T(8,128)(2,1)S(1)}, u32[]{:S(2)}, u32[]{:S(2)}) collective-permute-start(bf16[127,2048]{1,0:T(8,128)(2,1)S(1)} %slice.29), channel_id=1, source_target_pairs={{0,2},{2,4},{4,6},{6,8},{8,10},{10,12},{12,14},{14,16},{16,18},{18... | collective-permute-start | bytes 1560584 | tf_op jit(solution)/shard_map/ppermute | solution.py:15
  394.3 4.4 collective-permute-start.2
  437.5 1.0 copy-start.45
  437.5 1.2 copy-start.46
  437.7 3.6 copy-start.48
  440.0 23.0 %collective-permute-start = (bf16[127,2048]{1,0:T(8,128)(2,1)S(1)}, bf16[127,2048]{1,0:T(8,128)(2,1)S(1)}, u32[]{:S(2)}, u32[]{:S(2)}) collective-permute-start(bf16[127,2048]{1,0:T(8,128)(2,1)S(1)} %bitcast.393), channel_id=1, source_target_pairs={{2,0},{4,2},{6,4},{8,6},{10,8},{12,10},{14,12},{16,14},{18,16},{20... | collective-permute-start | bytes 1560584 | tf_op jit(solution)/shard_map/ppermute | solution.py:15
  463.2 16.6 %copy-start.49 = (bf16[1,134,2048]{2,1,0:T(8,128)(2,1)S(1)}, bf16[1,134,2048]{2,1,0:T(8,128)(2,1)}, u32[]{:S(2)}) copy-start(bf16[1,134,2048]{2,1,0:T(8,128)(2,1)} %maximum_bitcast_fusion.3) | copy-start | bytes 1646596
  478.4 97.0 %collective-permute-start.1 = (bf16[6,2048]{1,0:T(8,128)(2,1)S(1)}, bf16[6,2048]{1,0:T(8,128)(2,1)S(1)}, u32[]{:S(2)}, u32[]{:S(2)}) collective-permute-start(bf16[6,2048]{1,0:T(8,128)(2,1)S(1)} %bitcast.397), channel_id=1, source_target_pairs={{2,0},{4,2},{6,4},{8,6},{10,8},{12,10},{14,12},{16,14},{18,16},{20... | collective-permute-start | bytes 73736 | tf_op jit(solution)/shard_map/ppermute | solution.py:15
  575.5 0.8 copy-start.52
  (1 other events, 0.8 us)
Sparse Core Ops, SparseCore 0:
  9.5 29.1 all-gather.2
  41.5 145.4 all-gather.4
  463.2 109.9 all-reduce.1
where the time goes:
time: 593 us; the launch traced here: 585 us
  matrix products  200 us (34%)
  waiting for transfers between devices  145 us (24%)
  blocking collectives  93 us (16%)
  local copies, waits for them, and re-layouts  73.2 us (12%)
  starting transfers between devices  37 us (6%)
  other arithmetic  21.5 us (4%)
  between operations  15.2 us (3%)
    dot_general x66, matrix products, multiply(): return jnp.einsum(pattern, left, right, precision=ACCURATE)  154 us
    psum x1, blocking collectives, per_device(): sum_medium, sum_short = lax.psum((partial_medium, partial_short), 'seq')  68.9 us
    all_gather x1, waiting for transfers between devices, per_device(): lax.all_gather(aligned, 'seq', axis=0, tiled=True)  56.4 us
    conv_general_dilated x4, matrix products, depthwise(): lax.conv_general_dilated(signal.astype(jnp.float32)[None], kernel.astype(...  32.9 us
    unnamed x135, local copies, waits for them, and re-layouts  31.9 us
    all_to_all x1, waiting for transfers between devices, per_device(): lax.all_to_all(jnp.stack(results), 'seq', split_axis=1, concat_axis=1, ti...  30.2 us
    all_to_all x1, blocking collectives, per_device(): lax.all_to_all(out_weight, 'ch', split_axis=1, concat_axis=0, tiled=True)  24.2 us
    all_to_all x1, waiting for transfers between devices, per_device(): lax.all_to_all(to_blocks(product), 'seq', split_axis=0, concat_axis=0, ti...  21.9 us
  transfers between devices with their start and end apart: 11, of which 6 were waited for; matrix products, arithmetic and copies ran while one was open for 19% of the time, Pallas kernels for 0%

commit v1 on v0

--- a/solution.py
+++ b/solution.py
@@ -153,6 +153,35 @@
     taps_short,
     taps_medium,
 ):
+
+    def define_point(z_in, along_dim):
+        part_now, placed, v_now = (lax.psum(1, "seq"), lax.axis_index("seq"), z_in.shape[along_dim])
+        k_now = front = z_in
+        y1 = lax.dynamic_update_slice_in_dim(
+            jnp.zeros(
+                [jj * part_now if j0 == along_dim else jj for j0, jj in enumerate(z_in.shape)],
+                z_in.dtype,
+            ),
+            z_in,
+            placed * v_now,
+            axis=along_dim,
+        )
+        for tick in [*range(1, part_now // 2 + 1)]:
+            k_now = lax.ppermute(
+                k_now, "seq", [(j0, (j0 + 1) % part_now) for j0 in range(part_now)]
+            )
+            y1 = lax.dynamic_update_slice_in_dim(
+                y1, k_now, (placed - tick) % part_now * v_now, axis=along_dim
+            )
+            if 2 * tick < part_now:
+                front = lax.ppermute(
+                    front, "seq", [(j0, (j0 - 1) % part_now) for j0 in range(part_now)]
+                )
+                y1 = lax.dynamic_update_slice_in_dim(
+                    y1, front, (placed + tick) % part_now * v_now, axis=along_dim
+                )
+        return y1
+
     height = out_grad.shape[0]
     channels = outer_gate.shape[1]
     devices = lax.axis_size("seq")
@@ -162,11 +191,7 @@
     )
     features = lax.all_gather(out_grad, "ch", axis=1, tiled=True)
     aligned = lax.all_to_all(out_weight, "ch", split_axis=1, concat_axis=0, tiled=True)
-    hidden = jnp.dot(
-        features,
-        lax.all_gather(aligned, "seq", axis=0, tiled=True),
-        preferred_element_type=jnp.float32,
-    )
+    hidden = jnp.dot(features, define_point(aligned, 0), preferred_element_type=jnp.float32)
     grad_outer = (hidden * long_out.astype(jnp.float32)).astype(jnp.bfloat16)
     long_grad = (hidden * outer_gate.astype(jnp.float32)).astype(jnp.bfloat16)
     product = (inner_gate.astype(jnp.float32) * medium_out.astype(jnp.float32)).astype(jnp.bfloat16)

time: 593 us -> 665 us (1.12)
  starting transfers between devices: 37 us -> 128 us
  waiting for transfers between devices: 145 us -> 58.3 us
  local copies, waits for them, and re-layouts: 73.2 us -> 118 us
  matrix products: 200 us -> 221 us
    ppermute x0 -> x15, starting transfers between devices: none -> 77 us  [the longest x8 48.4 us: define_point(): lax.ppermute(k_now, 'seq', [(j0, (j0 + 1) % part_now) for j0 in range(par...]
    all_gather x1 -> x0, waiting for transfers between devices: 56.4 us -> none  [per_device(): lax.all_gather(aligned, 'seq', axis=0, tiled=True)]
    dynamic_update_slice x0 -> x16, local copies, waits for them, and re-layouts: none -> 25.8 us  [the longest x8 13.5 us: define_point(): lax.dynamic_update_slice_in_dim(y1, k_now, (placed - tick) % part_now * v...]
    all_to_all x1, waiting for transfers between devices: 21.9 us -> 0.01 us  [per_device(): lax.all_to_all(to_blocks(product), 'seq', split_axis=0, concat_axis=0, ti...]
    dot_general x66, matrix products: 154 us -> 170 us  [multiply(): return jnp.einsum(pattern, left, right, precision=ACCURATE)]
    all_to_all x1, waiting for transfers between devices: 13.7 us -> 0.01 us  [per_device(): lax.all_to_all(to_blocks(long_filter), 'seq', split_axis=0, concat_axis=0...]
    ppermute x0 -> x15, waiting for transfers between devices: none -> 12.7 us  [the longest x8 12.7 us: define_point(): lax.ppermute(k_now, 'seq', [(j0, (j0 + 1) % part_now) for j0 in range(par...]
    unnamed x135 -> x60, local copies, waits for them, and re-layouts: 31.9 us -> 44.6 us
  transfers between devices with their start and end apart: 11 -> 25, of which waited for: 6 -> 4; matrix products, arithmetic and copies ran while one was open for 19% -> 24% of each run, Pallas kernels for 0% -> 0%
where the time goes in v1:
time: 665 us; the launch traced here: 655 us
  matrix products  221 us (33%)
  starting transfers between devices  128 us (19%)
  local copies, waits for them, and re-layouts  118 us (18%)
  blocking collectives  88.6 us (13%)
  waiting for transfers between devices  58.3 us (9%)
  other arithmetic  25.8 us (4%)
  between operations  15.6 us (2%)
    dot_general x66, matrix products, multiply(): return jnp.einsum(pattern, left, right, precision=ACCURATE)  170 us
    psum x1, blocking collectives, per_device(): sum_medium, sum_short = lax.psum((partial_medium, partial_short), 'seq')  70.9 us
    ppermute x8, starting transfers between devices, define_point(): lax.ppermute(k_now, 'seq', [(j0, (j0 + 1) % part_now) for j0 in range(par...  48.4 us
    unnamed x60, local copies, waits for them, and re-layouts  44.6 us
    conv_general_dilated x4, matrix products, depthwise(): lax.conv_general_dilated(signal.astype(jnp.float32)[None], kernel.astype(...  34.5 us
    ppermute x7, starting transfers between devices, define_point(): lax.ppermute(front, 'seq', [(j0, (j0 - 1) % part_now) for j0 in range(par...  28.6 us
    all_to_all x1, waiting for transfers between devices, per_device(): lax.all_to_all(jnp.stack(results), 'seq', split_axis=1, concat_axis=1, ti...  26 us
    psum x1, waiting for transfers between devices, per_device(): sum_medium, sum_short = lax.psum((partial_medium, partial_short), 'seq')  18.7 us
  transfers between devices with their start and end apart: 25, of which 4 were waited for; matrix products, arithmetic and copies ran while one was open for 24% of the time, Pallas kernels for 0%

profile of v1, /device:TPU:0, one launch (start us, length us, event | category | flops | bytes accessed | tf_op | source)
XLA Modules:
  0.0 654.8 jit_solution(12147143209121941803)
XLA Ops:
  8.9 17.7 %all_to_all.63 = bf16[128,2,2048]{0,2,1:T(8,128)(2,1)S(1)} all-to-all(bf16[128,2,2048]{0,2,1:T(8,128)(2,1)S(1)} %bitcast.385), channel_id=1, replica_groups=mesh['seq'=16,'ch'=2] {'ch'}, dimensions={1} | all-to-all | bytes 2097152 | tf_op jit(solution)/shard_map/all_to_all | solution.py:193
  27.1 4.4 collective-permute-start.1
  31.5 12.7 %collective-permute-done = bf16[256,2048]{1,0:T(8,128)(2,1)} collective-permute-done((bf16[256,2048]{1,0:T(8,128)(2,1)S(1)}, bf16[256,2048]{1,0:T(8,128)(2,1)}, u32[]{:S(2)}, u32[]{:S(2)}) %collective-permute-start) | collective-permute-done | bytes 1048608 | tf_op jit(solution)/shard_map/ppermute | solution.py:170
  44.2 7.6 %collective-permute-start.2 = (bf16[256,2048]{1,0:T(8,128)(2,1)}, bf16[256,2048]{1,0:T(8,128)(2,1)}, u32[]{:S(2)}, u32[]{:S(2)}) collective-permute-start(bf16[256,2048]{1,0:T(8,128)(2,1)} %collective-permute-done), channel_id=1, source_target_pairs={{0,2},{2,4},{4,6},{6,8},{8,10},{10,12},{12,14},{14,16},{16,18},{18... | collective-permute-start | bytes 3145736 | tf_op jit(solution)/shard_map/ppermute | solution.py:170
  54.0 3.8 reduce.2
  59.0 7.2 %all-to-all-start.3 = ((bf16[16,2,8192]{2,1,0:T(2,128)(2,1)}), bf16[16,2,8192]{2,1,0:T(2,128)(2,1)S(1)}, u32[]{:S(2)}, u32[]{:S(2)}) async-start(bf16[16,2,8192]{2,1,0:T(2,128)(2,1)} %reshape.315), calls=%async_computation.3 | async-start | bytes 1048576 | tf_op jit(solution)/shard_map/all_to_all | solution.py:214
  66.1 4.4 collective-permute-start.3
  74.5 4.6 reduce
  81.3 14.6 %all-to-all-start.1 = ((bf16[16,2,8192]{2,1,0:T(2,128)(2,1)}), bf16[16,2,8192]{2,1,0:T(2,128)(2,1)}, u32[]{:S(2)}, u32[]{:S(2)}) async-start(bf16[16,2,8192]{2,1,0:T(2,128)(2,1)} %reshape.319), calls=%async_computation.1 | async-start | bytes 1048576 | tf_op jit(solution)/shard_map/all_to_all | solution.py:216
  96.0 4.3 collective-permute-start.5
  105.3 6.0 broadcast_in_dim.16
  116.3 4.1 fusion.65
  120.4 10.9 %collective-permute-start.7 = (bf16[256,2048]{1,0:T(8,128)(2,1)}, bf16[256,2048]{1,0:T(8,128)(2,1)S(1)}, u32[]{:S(2)}, u32[]{:S(2)}) collective-permute-start(bf16[256,2048]{1,0:T(8,128)(2,1)} %collective-permute-done.5), channel_id=1, source_target_pairs={{0,30},{2,0},{4,2},{6,4},{8,6},{10,8},{12,10},{14,12},{16,14},{18,... | collective-permute-start | bytes 3145736 | tf_op jit(solution)/shard_map/ppermute | solution.py:177
  131.4 5.1 fusion.58
  136.6 5.2 fusion.71
  141.8 5.1 fusion.56
  146.9 4.0 convolution_add_fusion.1
  151.0 4.5 collective-permute-start.9
  156.9 8.8 %collective-permute-start.10 = (bf16[256,2048]{1,0:T(8,128)(2,1)S(1)}, bf16[256,2048]{1,0:T(8,128)(2,1)S(1)}, u32[]{:S(2)}, u32[]{:S(2)}) collective-permute-start(bf16[256,2048]{1,0:T(8,128)(2,1)S(1)} %collective-permute-done.8), channel_id=1, source_target_pairs={{0,2},{2,4},{4,6},{6,8},{8,10},{10,12},{12,14},{14,16},{16,18},{18... | collective-permute-start | bytes 3145736 | tf_op jit(solution)/shard_map/ppermute | solution.py:170
  176.4 14.5 %collective-permute-start.12 = (bf16[256,2048]{1,0:T(8,128)(2,1)S(1)}, bf16[256,2048]{1,0:T(8,128)(2,1)S(1)}, u32[]{:S(2)}, u32[]{:S(2)}) collective-permute-start(bf16[256,2048]{1,0:T(8,128)(2,1)S(1)} %collective-permute-done.10), channel_id=1, source_target_pairs={{0,2},{2,4},{4,6},{6,8},{8,10},{10,12},{12,14},{14,16},{16,18},{18... | collective-permute-start | bytes 3145736 | tf_op jit(solution)/shard_map/ppermute | solution.py:170
  200.1 16.8 %collective-permute-start.14 = (bf16[256,2048]{1,0:T(8,128)(2,1)S(1)}, bf16[256,2048]{1,0:T(8,128)(2,1)S(1)}, u32[]{:S(2)}, u32[]{:S(2)}) collective-permute-start(bf16[256,2048]{1,0:T(8,128)(2,1)S(1)} %collective-permute-done.12), channel_id=1, source_target_pairs={{0,2},{2,4},{4,6},{6,8},{8,10},{10,12},{12,14},{14,16},{16,18},{18... | collective-permute-start | bytes 3145736 | tf_op jit(solution)/shard_map/ppermute | solution.py:170
  223.2 11.8 %multiply_convert_fusion = (bf16[128,2048]{0,1:T(8,128)(2,1)}, bf16[128,2048]{0,1:T(8,128)(2,1)}) fusion(bf16[128,2048]{0,1:T(8,128)(2,1)} %copy.156, bf16[128,2048]{0,1:T(8,128)(2,1)S(1)} %copy-done.12, bf16[4096,2048]{1,0:T(8,128)(2,1)} %constant_dynamic-update-slice_fusion, bf16[128,4096]{1,0:T(8,128)(2,1)} %all-gather.2.cloned.1.call-done), kind=kOutput, calls=%fused_computation.155 | convolution fusion | flops 2149056512 | bytes 19922944 | tf_op jit(solution)/shard_map/dot_general | solution.py:194
  238.0 4.9 reduce.1
  244.1 14.7 %all-to-all-start.2 = ((bf16[16,2,8192]{2,1,0:T(2,128)(2,1)}), bf16[16,2,8192]{2,1,0:T(2,128)(2,1)S(1)}, u32[]{:S(2)}, u32[]{:S(2)}) async-start(bf16[16,2,8192]{2,1,0:T(2,128)(2,1)} %reshape.317), calls=%async_computation.2 | async-start | bytes 1048576 | tf_op jit(solution)/shard_map/all_to_all | solution.py:215
  260.2 6.5 convolution_add_fusion.4
  266.7 6.5 convolution_subtract_fusion.1
  273.2 6.5 convolution_subtract_fusion.5
  283.6 4.0 fusion.57
  287.6 4.1 fusion.68
  292.7 4.3 convolution_subtract_fusion.4
  297.0 4.1 convolution_add_fusion.3
  301.1 11.2 %subtract_bitcast_fusion.6 = (f32[2,8,128,128]{3,1,2,0:T(8,128)}, f32[2,8,128,128]{3,1,2,0:T(8,128)}, f32[2,8,128,128]{3,1,2,0:T(8,128)}, f32[2,8,128,128]{3,1,2...) fusion(f32[16,16384]{1,0:T(8,128)} %convolution_add_fusion.4, ...), kind=kOutput, calls=%fused_computation.140 | convolution fusion | flops 38538752 | bytes 24707072 | tf_op jit(solution)/shard_map/ca,am->cm/dot_general | solution.py:32
  314.6 2.4 copy.222
  319.4 3.0 convolution_subtract_fusion.10
  327.8 2.4 copy.212
  333.6 3.0 convolution_subtract_fusion.15
  336.6 2.4 copy.209
  342.4 2.4 copy.210
  351.3 5.0 multiply_add_fusion.3
  363.3 2.4 copy.226
  368.1 3.1 convolution_subtract_fusion.8
  376.5 2.4 copy.218
  382.3 3.0 convolution_subtract_fusion.12
  385.3 2.4 copy.215
  391.3 2.4 copy.216
  400.3 3.5 multiply_add_fusion.2
  414.8 5.7 add_bitcast_fusion.4
  422.9 4.6 fusion.9
  431.3 4.4 fusion.4
  439.6 4.5 fusion.8
  444.1 4.7 fusion.3
  448.9 3.0 copy.179
  451.9 6.0 all-to-all-start.4
  462.2 3.5 collective-permute-start.17
  472.8 26.0 %all-to-all-done.4 = f32[2,16,16384]{2,0,1:T(2,128)S(1)} async-done(((f32[2,16,16384]{2,0,1:T(2,128)}), f32[2,16,16384]{2,0,1:T(2,128)S(1)}, u32[]{:S(2)}, u32[]{:S(2)}) %all-to-all-start.4) | async-done | bytes 2097184 | tf_op jit(solution)/shard_map/all_to_all | solution.py:227
  498.8 2.8 reshape.304
  501.6 2.8 copy.309
  504.7 2.6 fusion.19
  508.5 16.4 %fusion.11 = f32[1,128,2048]{2,0,1:T(1,128)S(1)} fusion(bf16[1,255,2048]{2,1,0:T(8,128)(2,1)} %maximum_bitcast_fusion.1, bf16[128,1,2048]{2,0,1:T(8,128)(2,1)} %bitcast.64), kind=kOutput, calls=%fused_computation.48 | convolution fusion | flops 67108864 | bytes 2617344 | tf_op jit(solution)/shard_map/conv_general_dilated | solution.py:123
  525.2 5.2 rev.7
  532.9 14.8 %convolution_convert_fusion = bf16[1,128,2048]{2,0,1:T(2,128)(2,1)S(1)} fusion(bf16[1,255,2048]{2,1,0:T(8,128)(2,1)S(1)} %maximum_bitcast_fusion, bf16[128,1,2048]{2,0,1:T(8,128)(2,1)S(1)} %bitcast.331), kind=kOutput, calls=%fused_computation.44 | convolution fusion | flops 67371008 | bytes 2093056 | tf_op jit(solution)/shard_map/conv_general_dilated | solution.py:123
  549.5 2.5 fusion.15
  552.4 70.9 %psum.14 = f32[7,2048]{1,0:T(8,128)S(1)} all-reduce(f32[7,2048]{1,0:T(8,128)S(1)} %rev.6), channel_id=1, replica_groups=mesh['seq'=16,'ch'=2] {'seq'}, use_global_device_ids=true, to_apply=%region_0.1 | all-reduce | flops 14336 | bytes 114688 | tf_op jit(solution)/shard_map/psum | solution.py:248
  623.9 18.7 %all-reduce.2.cloned.1.call-done = f32[128,2048]{1,0:T(8,128)} async-done(((f32[128,2048]{1,0:T(8,128)}), f32[128,2048]{1,0:T(8,128)}) %all-reduce.2.cloned.1.call-update) | async-done | bytes 1048592 | tf_op jit(solution)/shard_map/psum | solution.py:248
  (196 shorter events, 155.5 us)
Async XLA Ops:
  7.2 525.7 %copy-start = (bf16[128,2048]{1,0:T(8,128)(2,1)S(1)}, bf16[128,2048]{1,0:T(8,128)(2,1)}, u32[]{:S(2)}) copy-start(bf16[128,2048]{1,0:T(8,128)(2,1)} %param.21) | copy-start | bytes 1572868
  27.0 17.2 %collective-permute-start = (bf16[256,2048]{1,0:T(8,128)(2,1)S(1)}, bf16[256,2048]{1,0:T(8,128)(2,1)}, u32[]{:S(2)}, u32[]{:S(2)}) collective-permute-start(bf16[256,2048]{1,0:T(8,128)(2,1)S(1)} %bitcast.365), channel_id=1, source_target_pairs={{0,2},{2,4},{4,6},{6,8},{8,10},{10,12},{12,14},{14,16},{16,18},{18... | collective-permute-start | bytes 3145736 | tf_op jit(solution)/shard_map/ppermute | solution.py:170
  27.1 39.0 %collective-permute-start.1 = (bf16[256,2048]{1,0:T(8,128)(2,1)S(1)}, bf16[256,2048]{1,0:T(8,128)(2,1)}, u32[]{:S(2)}, u32[]{:S(2)}) collective-permute-start(bf16[256,2048]{1,0:T(8,128)(2,1)S(1)} %bitcast.366), channel_id=1, source_target_pairs={{0,30},{2,0},{4,2},{6,4},{8,6},{10,8},{12,10},{14,12},{16,14},{18,... | collective-permute-start | bytes 3145736 | tf_op jit(solution)/shard_map/ppermute | solution.py:177
  44.2 26.3 %collective-permute-start.2 = (bf16[256,2048]{1,0:T(8,128)(2,1)}, bf16[256,2048]{1,0:T(8,128)(2,1)}, u32[]{:S(2)}, u32[]{:S(2)}) collective-permute-start(bf16[256,2048]{1,0:T(8,128)(2,1)} %collective-permute-done), channel_id=1, source_target_pairs={{0,2},{2,4},{4,6},{6,8},{8,10},{10,12},{12,14},{14,16},{16,18},{18... | collective-permute-start | bytes 3145736 | tf_op jit(solution)/shard_map/ppermute | solution.py:170
  59.0 22.4 %all-to-all-start.3 = ((bf16[16,2,8192]{2,1,0:T(2,128)(2,1)}), bf16[16,2,8192]{2,1,0:T(2,128)(2,1)S(1)}, u32[]{:S(2)}, u32[]{:S(2)}) async-start(bf16[16,2,8192]{2,1,0:T(2,128)(2,1)} %reshape.315), calls=%async_computation.3 | async-start | bytes 1048576 | tf_op jit(solution)/shard_map/all_to_all | solution.py:214
  66.1 29.9 %collective-permute-start.3 = (bf16[256,2048]{1,0:T(8,128)(2,1)}, bf16[256,2048]{1,0:T(8,128)(2,1)}, u32[]{:S(2)}, u32[]{:S(2)}) collective-permute-start(bf16[256,2048]{1,0:T(8,128)(2,1)} %collective-permute-done.1), channel_id=1, source_target_pairs={{0,30},{2,0},{4,2},{6,4},{8,6},{10,8},{12,10},{14,12},{16,14},{18,... | collective-permute-start | bytes 3145736 | tf_op jit(solution)/shard_map/ppermute | solution.py:177
  70.5 29.9 %collective-permute-start.4 = (bf16[256,2048]{1,0:T(8,128)(2,1)}, bf16[256,2048]{1,0:T(8,128)(2,1)}, u32[]{:S(2)}, u32[]{:S(2)}) collective-permute-start(bf16[256,2048]{1,0:T(8,128)(2,1)} %collective-permute-done.2), channel_id=1, source_target_pairs={{0,2},{2,4},{4,6},{6,8},{8,10},{10,12},{12,14},{14,16},{16,18},{18... | collective-permute-start | bytes 3145736 | tf_op jit(solution)/shard_map/ppermute | solution.py:170
  81.3 32.2 %all-to-all-start.1 = ((bf16[16,2,8192]{2,1,0:T(2,128)(2,1)}), bf16[16,2,8192]{2,1,0:T(2,128)(2,1)}, u32[]{:S(2)}, u32[]{:S(2)}) async-start(bf16[16,2,8192]{2,1,0:T(2,128)(2,1)} %reshape.319), calls=%async_computation.1 | async-start | bytes 1048576 | tf_op jit(solution)/shard_map/all_to_all | solution.py:216
  96.0 127.3 %all-gather.2.cloned.1.call-start = ((), (), s32[]{:S(2)}) async-start(), calls=%async_computation.5 | async-start | bytes 1572864 | tf_op jit(solution)/shard_map/all_gather | solution.py:192
  96.0 24.4 %collective-permute-start.5 = (bf16[256,2048]{1,0:T(8,128)(2,1)}, bf16[256,2048]{1,0:T(8,128)(2,1)}, u32[]{:S(2)}, u32[]{:S(2)}) collective-permute-start(bf16[256,2048]{1,0:T(8,128)(2,1)} %collective-permute-done.3), channel_id=1, source_target_pairs={{0,30},{2,0},{4,2},{6,4},{8,6},{10,8},{12,10},{14,12},{16,14},{18,... | collective-permute-start | bytes 3145736 | tf_op jit(solution)/shard_map/ppermute | solution.py:177
  100.4 36.1 %collective-permute-start.6 = (bf16[256,2048]{1,0:T(8,128)(2,1)}, bf16[256,2048]{1,0:T(8,128)(2,1)}, u32[]{:S(2)}, u32[]{:S(2)}) collective-permute-start(bf16[256,2048]{1,0:T(8,128)(2,1)} %collective-permute-done.4), channel_id=1, source_target_pairs={{0,2},{2,4},{4,6},{6,8},{8,10},{10,12},{12,14},{14,16},{16,18},{18... | collective-permute-start | bytes 3145736 | tf_op jit(solution)/shard_map/ppermute | solution.py:170
  120.4 30.5 %collective-permute-start.7 = (bf16[256,2048]{1,0:T(8,128)(2,1)}, bf16[256,2048]{1,0:T(8,128)(2,1)S(1)}, u32[]{:S(2)}, u32[]{:S(2)}) collective-permute-start(bf16[256,2048]{1,0:T(8,128)(2,1)} %collective-permute-done.5), channel_id=1, source_target_pairs={{0,30},{2,0},{4,2},{6,4},{8,6},{10,8},{12,10},{14,12},{16,14},{18,... | collective-permute-start | bytes 3145736 | tf_op jit(solution)/shard_map/ppermute | solution.py:177
  136.5 20.4 %collective-permute-start.8 = (bf16[256,2048]{1,0:T(8,128)(2,1)}, bf16[256,2048]{1,0:T(8,128)(2,1)S(1)}, u32[]{:S(2)}, u32[]{:S(2)}) collective-permute-start(bf16[256,2048]{1,0:T(8,128)(2,1)} %collective-permute-done.6), channel_id=1, source_target_pairs={{0,2},{2,4},{4,6},{6,8},{8,10},{10,12},{12,14},{14,16},{16,18},{18... | collective-permute-start | bytes 3145736 | tf_op jit(solution)/shard_map/ppermute | solution.py:170
  151.0 23.2 %collective-permute-start.9 = (bf16[256,2048]{1,0:T(8,128)(2,1)S(1)}, bf16[256,2048]{1,0:T(8,128)(2,1)S(1)}, u32[]{:S(2)}, u32[]{:S(2)}) collective-permute-start(bf16[256,2048]{1,0:T(8,128)(2,1)S(1)} %collective-permute-done.7), channel_id=1, source_target_pairs={{0,30},{2,0},{4,2},{6,4},{8,6},{10,8},{12,10},{14,12},{16,14},{18,... | collective-permute-start | bytes 3145736 | tf_op jit(solution)/shard_map/ppermute | solution.py:177
  156.9 66.3 %copy-start.12 = (bf16[128,2048]{0,1:T(8,128)(2,1)S(1)}, bf16[128,2048]{0,1:T(8,128)(2,1)}, u32[]{:S(2)}) copy-start(bf16[128,2048]{0,1:T(8,128)(2,1)} %copy.151) | copy-start | bytes 1572868
  156.9 19.5 %collective-permute-start.10 = (bf16[256,2048]{1,0:T(8,128)(2,1)S(1)}, bf16[256,2048]{1,0:T(8,128)(2,1)S(1)}, u32[]{:S(2)}, u32[]{:S(2)}) collective-permute-start(bf16[256,2048]{1,0:T(8,128)(2,1)S(1)} %collective-permute-done.8), channel_id=1, source_target_pairs={{0,2},{2,4},{4,6},{6,8},{8,10},{10,12},{12,14},{14,16},{16,18},{18... | collective-permute-start | bytes 3145736 | tf_op jit(solution)/shard_map/ppermute | solution.py:170
  174.1 24.9 %collective-permute-start.11 = (bf16[256,2048]{1,0:T(8,128)(2,1)S(1)}, bf16[256,2048]{1,0:T(8,128)(2,1)S(1)}, u32[]{:S(2)}, u32[]{:S(2)}) collective-permute-start(bf16[256,2048]{1,0:T(8,128)(2,1)S(1)} %collective-permute-done.9), channel_id=1, source_target_pairs={{0,30},{2,0},{4,2},{6,4},{8,6},{10,8},{12,10},{14,12},{16,14},{18,... | collective-permute-start | bytes 3145736 | tf_op jit(solution)/shard_map/ppermute | solution.py:177
  176.4 23.6 %collective-permute-start.12 = (bf16[256,2048]{1,0:T(8,128)(2,1)S(1)}, bf16[256,2048]{1,0:T(8,128)(2,1)S(1)}, u32[]{:S(2)}, u32[]{:S(2)}) collective-permute-start(bf16[256,2048]{1,0:T(8,128)(2,1)S(1)} %collective-permute-done.10), channel_id=1, source_target_pairs={{0,2},{2,4},{4,6},{6,8},{8,10},{10,12},{12,14},{14,16},{16,18},{18... | collective-permute-start | bytes 3145736 | tf_op jit(solution)/shard_map/ppermute | solution.py:170
  199.0 22.1 %collective-permute-start.13 = (bf16[256,2048]{1,0:T(8,128)(2,1)S(1)}, bf16[256,2048]{1,0:T(8,128)(2,1)S(1)}, u32[]{:S(2)}, u32[]{:S(2)}) collective-permute-start(bf16[256,2048]{1,0:T(8,128)(2,1)S(1)} %collective-permute-done.11), channel_id=1, source_target_pairs={{0,30},{2,0},{4,2},{6,4},{8,6},{10,8},{12,10},{14,12},{16,14},{18,... | collective-permute-start | bytes 3145736 | tf_op jit(solution)/shard_map/ppermute | solution.py:177
  200.1 22.1 %collective-permute-start.14 = (bf16[256,2048]{1,0:T(8,128)(2,1)S(1)}, bf16[256,2048]{1,0:T(8,128)(2,1)S(1)}, u32[]{:S(2)}, u32[]{:S(2)}) collective-permute-start(bf16[256,2048]{1,0:T(8,128)(2,1)S(1)} %collective-permute-done.12), channel_id=1, source_target_pairs={{0,2},{2,4},{4,6},{6,8},{8,10},{10,12},{12,14},{14,16},{16,18},{18... | collective-permute-start | bytes 3145736 | tf_op jit(solution)/shard_map/ppermute | solution.py:170
  244.1 35.7 %all-to-all-start.2 = ((bf16[16,2,8192]{2,1,0:T(2,128)(2,1)}), bf16[16,2,8192]{2,1,0:T(2,128)(2,1)S(1)}, u32[]{:S(2)}, u32[]{:S(2)}) async-start(bf16[16,2,8192]{2,1,0:T(2,128)(2,1)} %reshape.317), calls=%async_computation.2 | async-start | bytes 1048576 | tf_op jit(solution)/shard_map/all_to_all | solution.py:215
  340.6 4.2 copy-start.6
  346.3 14.6 %copy-start.9 = (f32[2,8,128,128]{3,1,2,0:T(8,128)S(1)}, f32[2,8,128,128]{3,1,2,0:T(8,128)}, u32[]{:S(2)}) copy-start(f32[2,8,128,128]{3,1,2,0:T(8,128)} %get-tuple-element.81) | copy-start | bytes 3145732
  356.3 4.8 copy-start.1
  389.3 4.4 copy-start.5
  395.3 12.0 %copy-start.3 = (f32[128,2048]{1,0:T(8,128)S(1)}, f32[128,2048]{1,0:T(8,128)}, u32[]{:S(2)}) copy-start(f32[128,2048]{1,0:T(8,128)} %get-tuple-element.69) | copy-start | bytes 3145732
  395.3 12.9 %copy-start.4 = (f32[128,2048]{1,0:T(8,128)S(1)}, f32[128,2048]{1,0:T(8,128)}, u32[]{:S(2)}) copy-start(f32[128,2048]{1,0:T(8,128)} %get-tuple-element.68) | copy-start | bytes 3145732
  403.8 11.0 %copy-start.2 = (f32[128,2048]{1,0:T(8,128)S(1)}, f32[128,2048]{1,0:T(8,128)}, u32[]{:S(2)}) copy-start(f32[128,2048]{1,0:T(8,128)} %copy-done.1) | copy-start | bytes 3145732
  403.8 11.0 %copy-start.7 = (f32[128,2048]{1,0:T(8,128)S(1)}, f32[128,2048]{1,0:T(8,128)}, u32[]{:S(2)}) copy-start(f32[128,2048]{1,0:T(8,128)} %convolution_add_fusion.12) | copy-start | bytes 3145732
  403.8 11.0 %copy-start.8 = (f32[128,2048]{1,0:T(8,128)S(1)}, f32[128,2048]{1,0:T(8,128)}, u32[]{:S(2)}) copy-start(f32[128,2048]{1,0:T(8,128)} %fusion.195) | copy-start | bytes 3145732
  444.1 60.6 %copy-start.10 = (bf16[128,2048]{1,0:T(8,128)(2,1)S(1)}, bf16[128,2048]{1,0:T(8,128)(2,1)}, u32[]{:S(2)}) copy-start(bf16[128,2048]{1,0:T(8,128)(2,1)} %param.15) | copy-start | bytes 1572868
  451.9 47.0 %all-to-all-start.4 = ((f32[2,16,16384]{2,0,1:T(2,128)}), f32[2,16,16384]{2,0,1:T(2,128)S(1)}, u32[]{:S(2)}, u32[]{:S(2)}) async-start(f32[2,16,16384]{2,0,1:T(2,128)} %copy.179), calls=%async_computation.4 | async-start | bytes 4194304 | tf_op jit(solution)/shard_map/all_to_all | solution.py:227
  457.9 184.8 %all-reduce.2.cloned.1.call-start = ((), (), s32[]{:S(2)}) async-start(), calls=%async_computation.6 | async-start | bytes 2097152 | tf_op jit(solution)/shard_map/psum | solution.py:248
  459.1 9.5 %collective-permute-start.18 = (bf16[127,2048]{1,0:T(8,128)(2,1)S(1)}, bf16[127,2048]{1,0:T(8,128)(2,1)S(1)}, u32[]{:S(2)}, u32[]{:S(2)}) collective-permute-start(bf16[127,2048]{1,0:T(8,128)(2,1)S(1)} %slice.29), channel_id=1, source_target_pairs={{0,2},{2,4},{4,6},{6,8},{8,10},{10,12},{12,14},{14,16},{16,18},{18... | collective-permute-start | bytes 1560584 | tf_op jit(solution)/shard_map/ppermute | solution.py:15
  462.2 4.4 collective-permute-start.17
  507.2 24.6 %collective-permute-start.15 = (bf16[127,2048]{1,0:T(8,128)(2,1)}, bf16[127,2048]{1,0:T(8,128)(2,1)S(1)}, u32[]{:S(2)}, u32[]{:S(2)}) collective-permute-start(bf16[127,2048]{1,0:T(8,128)(2,1)} %bitcast.330), channel_id=1, source_target_pairs={{2,0},{4,2},{6,4},{8,6},{10,8},{12,10},{14,12},{16,14},{18,16},{20... | collective-permute-start | bytes 1560584 | tf_op jit(solution)/shard_map/ppermute | solution.py:15
  532.9 16.6 %copy-start.11 = (bf16[1,134,2048]{2,1,0:T(8,128)(2,1)S(1)}, bf16[1,134,2048]{2,1,0:T(8,128)(2,1)}, u32[]{:S(2)}) copy-start(bf16[1,134,2048]{2,1,0:T(8,128)(2,1)} %maximum_bitcast_fusion.3) | copy-start | bytes 1646596
  547.8 97.9 %copy-start.13 = (bf16[7,2048]{1,0:T(8,128)(2,1)S(1)}, bf16[7,2048]{1,0:T(8,128)(2,1)}, u32[]{:S(2)}) copy-start(bf16[7,2048]{1,0:T(8,128)(2,1)} %param.20) | copy-start | bytes 86020
  547.8 97.9 %copy-start.14 = (pred[8,17]{0,1:T(8,128)(4,1)S(1)}, pred[8,17]{0,1:T(8,128)(4,1)}, u32[]{:S(2)}) copy-start(pred[8,17]{0,1:T(8,128)(4,1)} %constant.228) | copy-start | bytes 412
  548.2 96.7 %collective-permute-start.16 = (bf16[6,2048]{1,0:T(8,128)(2,1)S(1)}, bf16[6,2048]{1,0:T(8,128)(2,1)S(1)}, u32[]{:S(2)}, u32[]{:S(2)}) collective-permute-start(bf16[6,2048]{1,0:T(8,128)(2,1)S(1)} %bitcast.394), channel_id=1, source_target_pairs={{2,0},{4,2},{6,4},{8,6},{10,8},{12,10},{14,12},{16,14},{18,16},{20... | collective-permute-start | bytes 73736 | tf_op jit(solution)/shard_map/ppermute | solution.py:15
Sparse Core Ops, SparseCore 0:
  100.5 19.4 all-gather.1
  530.6 112.0 all-reduce.1
